TPU v7x, 256 devices: a whole 4x4x8 slice. The times are simulated.
256 devices in a mesh: row: 16 (over x, z_lo), col: 16 (over y, z_hi, core).
Axes of the slice: x: 4, y: 4, z: 8 (z_hi: 2, z_lo: 4; z = z_hi * 4 + z_lo), core: 2. Of those that a mesh axis runs over, the one named last changes fastest.
Arguments:
- t2_amps: bfloat16 [16384, 49152], P('row', 'col'), may hold values from -0.5 to 0.5
- l2_amps: bfloat16 [512, 49152], P('row', 'col'), may hold values from -0.02734375 to 0.02734375
Outputs:
- ladder: bfloat16 [512, 49152], P('row', 'col')
All inputs are finite; a program needn't handle non-finite values.
Results may differ from a plain program's by a relative error of at most 0.0044.
Values may be sent and summed in bfloat16 or wider, within the bound.
A program may use at most 64 MiB of HBM per device.

v0:
```python
import jax
import jax.numpy as jnp
from jax import lax
from jax.sharding import Mesh
from jax.sharding import PartitionSpec as P

ROW = ("row_0", "row_1")
COL = ("col_0", "col_1", "col_2")


def in_blocks(value, dim, size):
    dims = value.shape
    parts = value.reshape(*dims[:dim], size, dims[dim] // size, *dims[dim + 1 :])
    return jnp.moveaxis(parts, dim, 0)


def sum_at_owner(value, axis, dim):
    parts = in_blocks(value, dim, lax.axis_size(axis))
    arrived = lax.all_to_all(parts, axis, split_axis=0, concat_axis=0, tiled=True)
    return arrived.sum(axis=0)


def sum_by_axis(value, axes, dim):
    far, near = axes
    own = sum_at_owner(in_blocks(value, dim, lax.axis_size(far)), near, dim + 1)
    return jnp.sum(lax.all_to_all(own, far, 0, 0, tiled=True), axis=0)


def padded_to(lines, size):
    spare = -lines.shape[0] % size
    if not spare:
        return lines
    return jnp.concatenate([lines, jnp.zeros((spare, *lines.shape[1:]), lines.dtype)])


def from_everyone(value, axis):
    size = lax.axis_size(axis)
    return lax.all_to_all(
        jnp.broadcast_to(value[None], (size, *value.shape)), axis, 0, 0, tiled=True
    )


def in_order(parts, dim):
    dims = list(parts.shape[1:])
    dims[dim] *= parts.shape[0]
    return jnp.moveaxis(parts, 0, dim).reshape(dims)


def gather_axes(value, axes, dim):
    far, near = axes
    initial = from_everyone(value, far)
    parts = jnp.swapaxes(from_everyone(initial, near), 0, 1)
    return in_order(parts.reshape(-1, *value.shape), dim)


def sum_by_parts(value, axes):
    lines = value.reshape(-1, value.shape[-1])
    own = sum_by_axis(padded_to(lines, lax.axis_size(axes[0]) * lax.axis_size(axes[1])), axes, 0)
    whole = gather_axes(own, axes, 0)
    return whole[: len(lines)].reshape(value.shape)


def own_rows(subtotal, axes):
    for axis in axes:
        subtotal = lax.psum_scatter(subtotal, axis, scatter_dimension=0, tiled=True)
    return subtotal


def on_device(t2_amps, l2_amps):
    partial_value = jnp.dot(
        t2_amps,
        lax.all_gather(l2_amps, ROW, axis=0, tiled=True).T,
        preferred_element_type=jnp.float32,
    )
    oooo = sum_by_parts(partial_value, (("col_0", "col_1"), "col_2"))
    oooo_half = oooo.astype(jnp.bfloat16)
    ladder = own_rows(
        lax.dot_general(
            oooo_half, t2_amps, (((0,), (0,)), ((), ())), preferred_element_type=jnp.float32
        ),
        ROW,
    )
    return ladder.astype(jnp.bfloat16)


def solution(mesh):
    finer = Mesh(mesh.devices.reshape(4, 4, 4, 2, 2), ("row_0", "row_1", "col_0", "col_1", "col_2"))
    return jax.shard_map(
        on_device,
        mesh=finer,
        in_specs=(P(ROW, COL), P(ROW, COL)),
        out_specs=P(ROW, COL),
        check_vma=False,
    )
```

profile of v0, /device:TPU:1, one launch (start us, length us, event | category | flops | bytes accessed | tf_op | source)
XLA Modules:
  0.0 296.4 jit_solution(4271393291127959320)
XLA Ops:
  6.5 0.0 all-gather.2.cloned.1.call-start
  6.5 0.7 all-gather.2.cloned.1.call-update
  7.3 0.0 reduce-scatter.3.cloned.1.call-start
  7.3 87.6 %all-gather.2.cloned.1.call-done = bf16[512,3072]{1,0:T(8,128)(2,1)} async-done(((bf16[32,3072]{1,0:T(8,128)(2,1)}), bf16[512,3072]{1,0:T(8,128)(2,1)}) %all-gather.2.cloned.1.call-update) | async-done | bytes 3145744 | tf_op jit(solution)/shard_map/all_gather | solution.py:72
  94.9 6.5 %fusion = f32[1024,512]{1,0:T(8,128)S(1)} fusion(bf16[1024,3072]{1,0:T(8,128)(2,1)} %param.2, bf16[512,3072]{1,0:T(8,128)(2,1)} %all-gather.2.cloned.1.call-done), kind=kOutput, calls=%fused_computation.2 | convolution fusion | flops 3221225472 | bytes 11534336 | tf_op jit(solution)/shard_map/dot_general | solution.py:70
  101.4 0.2 copy.10
  101.7 15.1 %all_to_all.20 = f32[2,8,64,512]{3,2,1,0:T(8,128)S(1)} all-to-all(f32[2,8,64,512]{3,2,1,0:T(8,128)S(1)} %bitcast.11), channel_id=1, replica_groups=mesh['row_0'=4,'row_1'=4,'col_0'=4,'col_1'=2,'col_2'=2] {'col_2'}, dimensions={0} | all-to-all | bytes 4194304 | tf_op jit(solution)/shard_map/all_to_all | solution.py:19
  116.8 0.3 reduce_sum.18
  117.1 33.2 %all_to_all.21 = f32[8,64,512]{2,1,0:T(8,128)S(1)} all-to-all(f32[8,64,512]{2,1,0:T(8,128)S(1)} %reduce_sum.18), channel_id=1, replica_groups=mesh['row_0'=4,'row_1'=4,'col_0'=4,'col_1'=2,'col_2'=2] {'col_0','col_1'}, dimensions={0} | all-to-all | bytes 2097152 | tf_op jit(solution)/shard_map/all_to_all | solution.py:26
  150.3 0.1 reduce_sum.19
  150.5 17.2 %all_to_all.22 = bf16[8,64,512]{2,1,0:T(8,128)(2,1)S(1)} all-to-all(bf16[8,64,512]{2,1,0:T(8,128)(2,1)S(1)} %broadcast_in_dim.4), channel_id=1, replica_groups=mesh['row_0'=4,'row_1'=4,'col_0'=4,'col_1'=2,'col_2'=2] {'col_0','col_1'}, dimensions={0} | all-to-all | bytes 1048576 | tf_op jit(solution)/shard_map/all_to_all | solution.py:38
  167.7 0.1 broadcast_in_dim.5
  167.8 7.5 %all_to_all.23 = bf16[2,8,64,512]{3,2,1,0:T(8,128)(2,1)S(1)} all-to-all(bf16[2,8,64,512]{3,2,1,0:T(8,128)(2,1)S(1)} %broadcast_in_dim.5), channel_id=1, replica_groups=mesh['row_0'=4,'row_1'=4,'col_0'=4,'col_1'=2,'col_2'=2] {'col_2'}, dimensions={0} | all-to-all | bytes 2097152 | tf_op jit(solution)/shard_map/all_to_all | solution.py:38
  175.3 0.1 copy.9
  175.4 8.2 %fusion.1 = f32[512,3072]{1,0:T(8,128)} fusion(bf16[1024,512]{1,0:T(8,128)(2,1)S(1)} %bitcast.12, bf16[1024,3072]{1,0:T(8,128)(2,1)} %param.2), kind=kOutput, calls=%fused_computation.3 | convolution fusion | flops 3221225472 | bytes 13631488 | tf_op jit(solution)/shard_map/dot_general | solution.py:78
  183.6 0.0 reduce-scatter.3.cloned.1.call-update
  183.6 0.0 reduce-scatter.5.cloned.1.call-start
  183.7 61.7 %reduce-scatter.3.cloned.1.call-done = f32[128,3072]{1,0:T(8,128)} async-done(((f32[512,3072]{1,0:T(8,128)}), f32[128,3072]{1,0:T(8,128)}) %reduce-scatter.3.cloned.1.call-update) | async-done | bytes 1572880 | tf_op jit(solution)/shard_map/reduce_scatter | solution.py:65
  245.4 0.0 reduce-scatter.5.cloned.1.call-update
  245.4 42.7 %reduce-scatter.5.cloned.1.call-done = f32[32,3072]{1,0:T(8,128)} async-done(((f32[128,3072]{1,0:T(8,128)}), f32[32,3072]{1,0:T(8,128)}) %reduce-scatter.5.cloned.1.call-update) | async-done | bytes 393232 | tf_op jit(solution)/shard_map/reduce_scatter | solution.py:65
  288.1 1.7 convert_element_type.15
  (1 shorter events, 0.0 us)
Async XLA Ops:
  6.5 88.4 %all-gather.2.cloned.1.call-start = ((), (), s32[]{:S(2)}) async-start(), calls=%async_computation.6 | async-start | bytes 3342336 | tf_op jit(solution)/shard_map/all_gather | solution.py:72
  7.3 238.1 %reduce-scatter.3.cloned.1.call-start = ((), (), s32[]{:S(2)}) async-start(), calls=%async_computation.7 | async-start | bytes 7864320 | tf_op jit(solution)/shard_map/reduce_scatter | solution.py:65
  183.6 104.5 %reduce-scatter.5.cloned.1.call-start = ((), (), s32[]{:S(2)}) async-start(), calls=%async_computation.8 | async-start | bytes 1966080 | tf_op jit(solution)/shard_map/reduce_scatter | solution.py:65
Sparse Core Ops, SparseCore 0:
  9.1 85.7 all-gather.1
  183.7 61.5 reduce-scatter.2
  247.9 40.1 reduce-scatter.4
where the time goes:
time: 297 us; the launch traced here: 296 us
  waiting for transfers between devices  193 us (65%)
  blocking collectives  73.1 us (25%)
  matrix products  14.7 us (5%)
  between operations  13.2 us (4%)
    reduce_scatter x2, waiting for transfers between devices, own_rows(): subtotal = lax.psum_scatter(subtotal, axis, scatter_dimension=0, tiled=True)  104 us
    all_gather x1, waiting for transfers between devices, on_device(): lax.all_gather(l2_amps, ROW, axis=0, tiled=True)  87.6 us
    all_to_all x1, blocking collectives, sum_by_axis(): return jnp.sum(lax.all_to_all(own, far, 0, 0, tiled=True), axis=0)  33.2 us
    all_to_all x2, blocking collectives, from_everyone(): lax.all_to_all(jnp.broadcast_to(value[None], (size, *value.shape)), axis,...  24.8 us
    all_to_all x1, blocking collectives, sum_at_owner(): lax.all_to_all(parts, axis, split_axis=0, concat_axis=0, tiled=True)  15.1 us
    dot_general x1, matrix products, on_device(): lax.dot_general(oooo_half, t2_amps, (((0,), (0,)), ((), ())), preferred_e...  8.19 us
    dot_general x1, matrix products, on_device(): jnp.dot(t2_amps, lax.all_gather(l2_amps, ROW, axis=0, tiled=True).T, pref...  6.51 us
  transfers between devices with their start and end apart: 3, of which 3 were waited for; matrix products, arithmetic and copies ran while one was open for 0% of the time, Pallas kernels for 0%

commit v1 on v0

v1 whole, which is shorter than its diff:
```python
import jax
import jax.numpy as jnp
from jax import lax
from jax.experimental import pallas as pl
from jax.experimental.pallas import tpu as pltpu
from jax.sharding import PartitionSpec as P

MESH = pl.DeviceIdType.MESH
F32, BF16 = jnp.float32, jnp.bfloat16

PARTS = 4
NX, NZ, NY = 4, 4, 4
STEP = 6.3
Z_TYPE = F32
R_TYPE = BF16


def kernel(
    t2_hbm, l2_hbm, out_ref,
    t2, g, p, rc, sy, ry, q, sz, rz, h, lad, xas, xa, xbs, xb, zs, zb,
    local, sems,
):
    rows, width = t2.shape
    piece = g.shape[2]
    row, col = lax.axis_index("row"), lax.axis_index("col")
    x, z = row // NZ, row % NZ
    y, zh, c = col // 4, (col // 2) % 2, col % 2

    def z_peer(d):
        return (x * NZ + (z + d) % NZ, col)

    def x_peer(d):
        return (((x + d) % NX) * NZ + z, col)

    def y_peer(d):
        return (row, ((y + d) % NY) * 4 + zh * 2 + c)

    far = (row, y * 4 + (1 - zh) * 2 + c)
    partner = (row, y * 4 + zh * 2 + (1 - c))

    load_t2 = pltpu.make_async_copy(t2_hbm, t2, local.at[0])
    load_t2.start()
    loads = []
    for j in range(PARTS):
        load = pltpu.make_async_copy(l2_hbm.at[pl.ds(j * piece, piece)], g.at[j, row], local.at[1 + j])
        load.start()
        loads.append(load)

    barrier = pltpu.get_barrier_semaphore()
    peers = [z_peer(1), z_peer(2), z_peer(3), x_peer(1), x_peer(3), y_peer(1), y_peer(2), y_peer(3), far, partner]
    for peer in peers:
        pl.semaphore_signal(barrier, inc=1, device_id=peer, device_id_type=MESH)
    pl.semaphore_wait(barrier, len(peers))

    names = {}
    sent = []

    def slot(name):
        return names.setdefault(name, len(names))

    def send(name, src, dst, device):
        k = slot(name)
        copy = pltpu.make_async_remote_copy(
            src_ref=src, dst_ref=dst, send_sem=sems.at[0, k], recv_sem=sems.at[1, k],
            device_id=device, device_id_type=MESH,
        )
        copy.start()
        sent.append(copy)

    def arrived(name, dst):
        k = slot(name)
        pltpu.make_async_remote_copy(
            src_ref=dst, dst_ref=dst, send_sem=sems.at[0, k], recv_sem=sems.at[1, k],
            device_id=partner, device_id_type=MESH,
        ).wait_recv()

    events = []

    def at(time):
        def add(f):
            events.append((time, len(events), f))
            return f

        return add

    def x_own(j):
        own = g.at[j, row]
        send(("x", j, 0, 0), own, own, x_peer(1))
        send(("x", j, 1, 0), own, own, x_peer(3))

    def chunk(j):
        base = j * STEP

        @at(0.0 + 0.001 * j)
        def _():
            loads[j].wait()
            own = g.at[j, row]
            if j == 0:
                x_own(j)
            for d in (1, 3, 2):
                send(("z", j, d), own, own, z_peer(d))

        @at(4.0 + base)
        def _():
            for d in (1, 3, 2):
                got = g.at[j, x * NZ + (z + NZ - d) % NZ]
                arrived(("z", j, d), got)
                send(("x", j, 0, d), got, got, x_peer(1))
                send(("x", j, 1, d), got, got, x_peer(3))
            if j + 1 < PARTS:
                x_own(j + 1)

        @at(8.0 + base)
        def _():
            for way, d in ((0, NX - 1), (1, 1)):
                group = ((x + d) % NX) * NZ
                for e in range(NZ):
                    arrived(("x", j, way, e), g.at[j, group + (z + NZ - e) % NZ])
                half = g.at[j, pl.ds(group + way * (NZ // 2), NZ // 2)]
                send(("relay", j, way), half, half, x_peer(1 if way == 0 else 3))

        m = 11.0 + base

        @at(m)
        def _():
            if j == 0:
                load_t2.wait()
            group = ((x + 2) % NX) * NZ
            for way in range(2):
                arrived(("relay", j, way), g.at[j, pl.ds(group + way * (NZ // 2), NZ // 2)])
            block = 256

            def one(n, _):
                at_n = pl.ds(pl.multiple_of(n * block, block), block)
                p[j, :, at_n] = lax.dot_general(
                    g[j].reshape(NX * NZ * piece, width), t2[at_n, :], (((1,), (1,)), ((), ())),
                    preferred_element_type=F32,
                )
                return _

            lax.fori_loop(0, rows // block, one, 0)
            half = p.shape[1] // 2
            send(("core", j), p.at[j, pl.ds((1 - c) * half, half)], rc.at[j], partner)

        @at(m + 3.5)
        def _():
            arrived(("core", j), rc.at[j])
            half = p.shape[1] // 2
            sy[j] = p[j, pl.ds(c * half, half), :] + rc[j]
            part = half // NY
            for d in (1, 3, 2):
                send(("y", j, d), sy.at[j, pl.ds(((y + d) % NY) * part, part)], ry.at[j, d - 1], y_peer(d))

        @at(m + 10.0)
        def _():
            part = q.shape[1]
            for d in (1, 3, 2):
                arrived(("y", j, d), ry.at[j, d - 1])
            total = sy[j, pl.ds(y * part, part), :] + ry[j, 0] + ry[j, 1] + ry[j, 2]
            q[j] = total
            sz[j] = total.astype(sz.dtype)
            send(("far", j), sz.at[j], rz.at[j], far)

        @at(m + 16.0)
        def _():
            part = q.shape[1]
            arrived(("far", j), rz.at[j])
            mine = pl.ds(c * (part * NY) + y * part, part)
            h[j, mine, :] = (q[j] + rz[j].astype(F32)).astype(BF16)
            own = h.at[j, mine]
            for d in (1, 3, 2):
                send(("ya", j, d), own, own, y_peer(d))

        @at(m + 20.0)
        def _():
            part = q.shape[1]
            for d in (1, 3, 2):
                arrived(("ya", j, d), h.at[j, pl.ds(c * (part * NY) + ((y + NY - d) % NY) * part, part)])
            own = h.at[j, pl.ds(c * (part * NY), part * NY)]
            send(("ca", j), own, own, partner)

        group_rows = NZ * piece
        half_rows = group_rows // 2

        def ladder_rows(group, half):
            return lad[j, pl.ds((group % NX) * group_rows + half * half_rows, half_rows), :]

        @at(m + 22.0)
        def _():
            part = q.shape[1]
            arrived(("ca", j), h.at[j, pl.ds((1 - c) * (part * NY), part * NY)])
            block = 512

            def one(n, _):
                at_n = pl.ds(pl.multiple_of(n * block, block), block)
                lad[j, :, at_n] = jnp.dot(h[j], t2[:, at_n], preferred_element_type=F32)
                return _

            lax.fori_loop(0, width // block, one, 0)
            for way in range(2):
                xas[j, way] = ladder_rows(x + 2, way).astype(BF16)
                send(("a", j, way), xas.at[j, way], xa.at[j, way], x_peer(1 if way == 0 else 3))
            for way in range(2):
                free = 1 - way
                xbs[j, way, free] = ladder_rows(x + (1 if way == 0 else 3), free).astype(BF16)
                send(("b", j, way, free), xbs.at[j, way, free], xb.at[j, way, free], x_peer(1 if way == 0 else 3))

        @at(m + 28.0)
        def _():
            for way in range(2):
                arrived(("a", j, way), xa.at[j, way])
                rows_ = ladder_rows(x + (1 if way == 0 else 3), way) + xa[j, way].astype(F32)
                xbs[j, way, way] = rows_.astype(BF16)
                send(("b", j, way, way), xbs.at[j, way, way], xb.at[j, way, way], x_peer(1 if way == 0 else 3))

        @at(m + 33.0)
        def _():
            for half in range(2):
                for way in range(2):
                    arrived(("b", j, way, half), xb.at[j, way, half])
                total = ladder_rows(x, half) + xb[j, 0, half].astype(F32) + xb[j, 1, half].astype(F32)
                lad[j, pl.ds(x * group_rows + half * half_rows, half_rows), :] = total
                for e in range(NZ // 2):
                    zs[j, half * (NZ // 2) + e] = total[e * piece : (e + 1) * piece].astype(zs.dtype)
            for d in (2, 1, 3):
                send(("zr", j, d), zs.at[j, (z + d) % NZ], zb.at[j, d - 1], z_peer(d))

        @at(m + 41.0)
        def _():
            for d in (1, 3, 2):
                arrived(("zr", j, d), zb.at[j, d - 1])
            total = lad[j, pl.ds(x * group_rows + z * piece, piece), :]
            for d in range(3):
                total += zb[j, d].astype(F32)
            out_ref[pl.ds(j * piece, piece), :] = total.astype(BF16)

    for j in range(PARTS):
        chunk(j)
    for _, _, event in sorted(events, key=lambda e: e[:2]):
        event()
    for copy in sent:
        copy.wait_send()


def on_device(t2_amps, l2_amps):
    rows, width = t2_amps.shape
    piece = l2_amps.shape[0] // PARTS
    kl = NX * NZ * piece
    part = kl // 2 // NY
    half = NZ * piece // 2
    return pl.pallas_call(
        kernel,
        out_shape=jax.ShapeDtypeStruct(l2_amps.shape, BF16),
        in_specs=[pl.BlockSpec(memory_space=pl.ANY)] * 2,
        out_specs=pl.BlockSpec(memory_space=pltpu.VMEM),
        scratch_shapes=[
            pltpu.VMEM((rows, width), BF16),
            pltpu.VMEM((PARTS, NX * NZ, piece, width), BF16),
            pltpu.VMEM((PARTS, kl, rows), F32),
            pltpu.VMEM((PARTS, kl // 2, rows), F32),
            pltpu.VMEM((PARTS, kl // 2, rows), F32),
            pltpu.VMEM((PARTS, NY - 1, part, rows), F32),
            pltpu.VMEM((PARTS, part, rows), F32),
            pltpu.VMEM((PARTS, part, rows), Z_TYPE),
            pltpu.VMEM((PARTS, part, rows), Z_TYPE),
            pltpu.VMEM((PARTS, kl, rows), BF16),
            pltpu.VMEM((PARTS, kl, width), F32),
            pltpu.VMEM((PARTS, 2, half, width), BF16),
            pltpu.VMEM((PARTS, 2, half, width), BF16),
            pltpu.VMEM((PARTS, 2, 2, half, width), BF16),
            pltpu.VMEM((PARTS, 2, 2, half, width), BF16),
            pltpu.VMEM((PARTS, NZ, piece, width), R_TYPE),
            pltpu.VMEM((PARTS, NZ - 1, piece, width), R_TYPE),
            pltpu.SemaphoreType.DMA((1 + PARTS,)),
            pltpu.SemaphoreType.DMA((2, 31 * PARTS)),
        ],
        compiler_params=pltpu.CompilerParams(
            collective_id=0, has_side_effects=True, vmem_limit_bytes=60 * 2**20
        ),
    )(t2_amps, l2_amps)


def solution(mesh):
    return jax.shard_map(
        on_device,
        mesh=mesh,
        in_specs=(P("row", "col"), P("row", "col")),
        out_specs=P("row", "col"),
        check_vma=False,
    )
```

time: 297 us -> 95.4 us (0.32)
  waiting for transfers between devices: 193 us -> 0 us
  Pallas kernels: 0 us -> 92.8 us
  blocking collectives: 73.1 us -> 0 us
  matrix products: 14.7 us -> 0 us
  between operations: 13.2 us -> 0.01 us
    reduce_scatter x2 -> x0, waiting for transfers between devices: 104 us -> none  [own_rows(): subtotal = lax.psum_scatter(subtotal, axis, scatter_dimension=0, tiled=True)]
    pallas_call x0 -> x1, Pallas kernels: none -> 92.8 us  [on_device(): pl.pallas_call(kernel, out_shape=jax.ShapeDtypeStruct(l2_amps.shape, BF16...]
    all_gather x1 -> x0, waiting for transfers between devices: 87.6 us -> none  [on_device(): lax.all_gather(l2_amps, ROW, axis=0, tiled=True)]
    all_to_all x4 -> x0, blocking collectives: 73.1 us -> none  [the longest x1 33.2 us: sum_by_axis(): return jnp.sum(lax.all_to_all(own, far, 0, 0, tiled=True), axis=0)]
    dot_general x2 -> x0, matrix products: 14.7 us -> none  [the longest x1 8.19 us: on_device(): lax.dot_general(oooo_half, t2_amps, (((0,), (0,)), ((), ())), preferred_e...]
  transfers between devices with their start and end apart: 3 -> 0, of which waited for: 3 -> 0; matrix products, arithmetic and copies ran while one was open for 0% -> 0% of each run, Pallas kernels for 0% -> 0%
where the time goes in v1:
time: 95.4 us; the launch traced here: 94.5 us
  Pallas kernels  92.8 us (97%)
  local copies, waits for them, and re-layouts  1.62 us (2%)
    pallas_call x1, Pallas kernels, on_device(): pl.pallas_call(kernel, out_shape=jax.ShapeDtypeStruct(l2_amps.shape, BF16...  92.8 us

profile of v1, /device:TPU:1, one launch (start us, length us, event | category | flops | bytes accessed | tf_op | source)
XLA Modules:
  0.0 94.5 jit_solution(11957673919986456872)
XLA Ops:
  0.0 92.8 %shard_map.28 = bf16[32,3072]{1,0:T(8,128)(2,1)} custom-call(bf16[1024,3072]{1,0:T(8,128)(2,1)} %t2_hbm.1, bf16[32,3072]{1,0:T(8,128)(2,1)} %l2_hbm.1), custom_call_target="tpu_custom_call" | custom-call | tf_op jit(solution)/shard_map/pallas_call | solution.py:251
  92.8 1.6 %copy.4 = bf16[32,3072]{1,0:T(8,128)(2,1)} copy(bf16[32,3072]{1,0:T(8,128)(2,1)} %shard_map.28) | data formatting | bytes 393216

commit v2 on v0

v2 whole, which is shorter than its diff:
```python
import jax
import jax.numpy as jnp
from jax import lax
from jax.experimental import pallas as pl
from jax.experimental.pallas import tpu as pltpu
from jax.sharding import PartitionSpec as P

MESH = pl.DeviceIdType.MESH
F32, BF16 = jnp.float32, jnp.bfloat16

PARTS = 4
CHUNKS = 2 * PARTS
NX, NZ, NY = 4, 4, 4
FAR_TYPE = BF16

ORDER = (
    "ob0 ox1 ox0 ox3",
    "oa0 f10 oa1 f30",
    "tt1 tt3 ox2 ob1",
    "tt0 f20 rl1 oa2",
    "tt2 f21 rl0 f31",
    "f11 ob2 ma1 rl2",
    "ys1 oa3 f22 ma0",
    "rl3 f32 ys0 ob3",
    "f12 ma2 rl4 yq1",
    "ys2 f23 ma3 yq0",
    "rl5 f13 f33 ys3",
    "ma4 rl6 yq2 zq1",
    "ys4 ma5 zq0 yq3",
    "rl7 ys5 ma6 zq2",
    "ca1 yq4 ys6 ca0",
    "ma7 mm0 ys7 yq5",
    "ca2 zq3 bf0 mm1",
    "mm2 yq6 zq4 bf2",
    "bd0 yq7 bf1 ca3",
    "zq5 bd1 ca4 bd2",
    "mm3 mm4 bs0 bf4",
    "zq6 ca5 zq7 bf3",
    "bs1 bd3 mm5 bd4",
    "bf5 ca6 ca7 bs2",
    "mm6 mm7 bs4 bd5",
    "ou0 bs3 bf6 bd6",
    "bf7 bs5 bd7 bs6",
    "bs7 ou2 ou1 ou3",
)


def kernel(
    t2_hbm, l2_hbm, out_hbm,
    t2, t2t, g, p, rc, sy, ry, q, sz, rz, h, lad, xas, xa, xbs, xb, zs, zb, out,
    local, send_sems, sems,
):
    rows, width = t2.shape
    piece = g.shape[3]
    kl = p.shape[1]
    half = kl // 2
    row, col = lax.axis_index("row"), lax.axis_index("col")
    x, z = row // NZ, row % NZ
    zz = z // 2
    y, zh, c = col // 4, (col // 2) % 2, col % 2

    def z_peer(d):
        return (x * NZ + (z + d) % NZ, col)

    def x_peer(way):
        return (((x + (1 if way == 0 else NX - 1)) % NX) * NZ + z, col)

    def y_peer(d):
        return (row, ((y + d) % NY) * 4 + zh * 2 + c)

    far = (row, y * 4 + (1 - zh) * 2 + c)
    partner = (row, y * 4 + zh * 2 + (1 - c))

    loads = []
    for j in range(PARTS):
        loads.append(pltpu.make_async_copy(l2_hbm.at[pl.ds(j * piece, piece)], g.at[2 * j, x, zz], local.at[j]))
    loads.append(pltpu.make_async_copy(t2_hbm, t2, local.at[PARTS]))
    for copy in loads:
        copy.start()

    barrier = pltpu.get_barrier_semaphore()
    peers = [z_peer(1), z_peer(2), z_peer(3), x_peer(0), x_peer(1), y_peer(1), y_peer(2), y_peer(3), far, partner]
    for peer in peers:
        pl.semaphore_signal(barrier, inc=1, device_id=peer, device_id_type=MESH)
    pl.semaphore_wait(barrier, len(peers))

    names = {}

    count = [0]

    def index(name, size=1):
        if name not in names:
            names[name] = count[0]
            count[0] += size
        return names[name]

    kinds = ("x", "z", "c", "y", "far", "ya", "ca", "a", "b", "zr")

    def send(kind, k, src, dst, device):
        pltpu.make_async_remote_copy(
            src_ref=src, dst_ref=dst, send_sem=send_sems.at[kinds.index(kind)], recv_sem=sems.at[k],
            device_id=device, device_id_type=MESH,
        ).start()

    def waiting(kind, k, ref):
        return pltpu.make_async_remote_copy(
            src_ref=ref, dst_ref=ref, send_sem=send_sems.at[kinds.index(kind)], recv_sem=sems.at[k],
            device_id=partner, device_id_type=MESH,
        )

    def arrived(k, ref):
        with jax.named_scope("w"):
            waiting("x", k, ref).wait_recv()

    def send_x(k, slot_z):
        block = g.at[k, x, slot_z]
        first = index(("x", k), 3)
        for way in range(2):
            send("x", first + jnp.where(slot_z == way, way, 2), block, block, x_peer(way))

    loaded = set()

    def load(j):
        if j not in loaded:
            loaded.add(j)
            loads[j].wait()

    def to_z(j, d):
        load(j)
        send("z", index(("z", j, d)), g.at[2 * j, x, zz], g.at[2 * j + d % 2, x, zz], z_peer(d))

    def oa(j):
        to_z(j, 2)

    def ob(j):
        to_z(j, 1)
        to_z(j, 3)

    def ox(j):
        load(j)
        send_x(2 * j, zz)

    def from_z(j, d):
        k, slot_z = 2 * j + d % 2, ((z + NZ - d) % NZ) // 2
        arrived(index(("z", j, d)), g.at[k, x, slot_z])
        send_x(k, slot_z)

    def f1(j):
        from_z(j, 1)

    def f2(j):
        from_z(j, 2)

    def f3(j):
        from_z(j, 3)

    def rl(k):
        for way in range(2):
            block = g.at[k, (x + (NX - 1 if way == 0 else 1)) % NX, way]
            arrived(index(("x", k), 3) + way, block)
            send("x", index(("x", k), 3) + 2, block, block, x_peer(way))

    def ma(k):
        arrived(index(("x", k), 3) + 2, g.at[k, pl.ds(0, 2)])
        columns = rows // 2
        for s in range(2):
            at_s = pl.ds(s * columns, columns)
            p[k, :, at_s] = jnp.dot(g[k].reshape(kl, width), t2t[:, at_s], preferred_element_type=F32)
            send("c", index(("c", k)), p.at[k, pl.ds((1 - c) * half, half), at_s], rc.at[k, :, at_s], partner)

    def tt(i):
        load(PARTS)
        size = rows // 4
        t2t[:, i * size : (i + 1) * size] = t2[i * size : (i + 1) * size, :].T

    def ys(k):
        arrived(index(("c", k)), rc.at[k])
        sy[k] = (p[k, pl.ds(c * half, half), :] + rc[k]).reshape(NY, half // NY, rows)
        for d in (2, 1, 3):
            send("y", index(("y", k)), sy.at[k, (y + d) % NY], ry.at[k, d - 1], y_peer(d))

    def yq(k):
        arrived(index(("y", k)), ry.at[k])
        total = sy[k, y] + ry[k, 0] + ry[k, 1] + ry[k, 2]
        q[k] = total
        sz[k] = total.astype(sz.dtype)
        send("far", index(("far", k)), sz.at[k], rz.at[k], far)

    def zq(k):
        arrived(index(("far", k)), rz.at[k])
        h[k, c, y] = (q[k] + rz[k].astype(F32)).astype(BF16)
        own = h.at[k, c, y]
        for d in (2, 1, 3):
            send("ya", index(("ya", k)), own, own, y_peer(d))

    def ca(k):
        arrived(index(("ya", k)), h.at[k, c, pl.ds(0, NY - 1)])
        own = h.at[k, c]
        send("ca", index(("ca", k)), own, own, partner)

    def ladder_rows(k, group, slot_z):
        return lad[k, pl.ds((group % NX) * (2 * piece) + slot_z * piece, piece), :]

    def mm(k):
        arrived(index(("ca", k)), h.at[k, 1 - c])
        lad[k] = jnp.dot(h[k].reshape(kl, rows), t2[...], preferred_element_type=F32)
        for way in range(2):
            xas[k, way] = ladder_rows(k, x + 2, way).astype(BF16)
            send("a", index(("a", k, way)), xas.at[k, way], xa.at[k, way], x_peer(way))

    def bf(k):
        for way in range(2):
            xbs[k, 1 - way, way] = ladder_rows(k, x + (1 if way == 0 else 3), 1 - way).astype(BF16)
            send("b", index(("b", k, 1 - way)), xbs.at[k, 1 - way, way], xb.at[k, 1 - way, way], x_peer(way))

    def bd(k):
        for way in range(2):
            arrived(index(("a", k, way)), xa.at[k, way])
            total = ladder_rows(k, x + (1 if way == 0 else 3), way) + xa[k, way].astype(F32)
            xbs[k, way, way] = total.astype(BF16)
            send("b", index(("b", k, way)), xbs.at[k, way, way], xb.at[k, way, way], x_peer(way))

    def bs(k):
        for slot_z in range(2):
            arrived(index(("b", k, slot_z)), xb.at[k, slot_z])
            total = ladder_rows(k, x, slot_z) + xb[k, slot_z, 0].astype(F32) + xb[k, slot_z, 1].astype(F32)
            if k % 2 == 0:
                lad[k, pl.ds(x * (2 * piece) + slot_z * piece, piece), :] = total
            zs[k, slot_z] = total.astype(BF16)
        for d in (2,) if k % 2 == 0 else (1, 3):
            send("zr", index(("zr", k // 2)), zs.at[k, ((z + d) % NZ) // 2], zb.at[k // 2, d - 1], z_peer(d))

    stores = []

    def ou(j):
        arrived(index(("zr", j)), zb.at[j])
        total = ladder_rows(2 * j, x, zz)
        for d in range(3):
            total += zb[j, d].astype(F32)
        out[j] = total.astype(BF16)
        store = pltpu.make_async_copy(out.at[j], out_hbm.at[pl.ds(j * piece, piece)], local.at[j])
        store.start()
        stores.append(store)

    events = dict(oa=oa, ob=ob, tt=tt, ox=ox, f1=f1, f2=f2, f3=f3, rl=rl, ma=ma, ys=ys, yq=yq, zq=zq, ca=ca, mm=mm, bf=bf, bd=bd, bs=bs, ou=ou)
    for name in " ".join(ORDER).split():
        with jax.named_scope(name):
            events[name[:2]](int(name[2:]))
    with jax.named_scope("drain"):
        sent = dict(
            x=g.at[pl.ds(0, 6)], z=zb, c=rc, y=ry, far=rz, ya=h.at[pl.ds(0, 3)], ca=h.at[pl.ds(0, 4)], a=xa, b=xb, zr=zb
        )
        for kind in kinds:
            waiting(kind, 0, sent[kind]).wait_send()
        for store in stores:
            store.wait()


def on_device(t2_amps, l2_amps):
    rows, width = t2_amps.shape
    piece = l2_amps.shape[0] // PARTS
    kl = NX * 2 * piece
    return pl.pallas_call(
        kernel,
        out_shape=jax.ShapeDtypeStruct(l2_amps.shape, BF16),
        in_specs=[pl.BlockSpec(memory_space=pl.ANY)] * 2,
        out_specs=pl.BlockSpec(memory_space=pl.ANY),
        scratch_shapes=[
            pltpu.VMEM((rows, width), BF16),
            pltpu.VMEM((width, rows), BF16),
            pltpu.VMEM((CHUNKS, NX, 2, piece, width), BF16),
            pltpu.VMEM((CHUNKS, kl, rows), F32),
            pltpu.VMEM((CHUNKS, kl // 2, rows), F32),
            pltpu.VMEM((CHUNKS, NY, kl // 2 // NY, rows), F32),
            pltpu.VMEM((CHUNKS, NY - 1, kl // 2 // NY, rows), F32),
            pltpu.VMEM((CHUNKS, kl // 2 // NY, rows), F32),
            pltpu.VMEM((CHUNKS, kl // 2 // NY, rows), FAR_TYPE),
            pltpu.VMEM((CHUNKS, kl // 2 // NY, rows), FAR_TYPE),
            pltpu.VMEM((CHUNKS, 2, NY, kl // 2 // NY, rows), BF16),
            pltpu.VMEM((CHUNKS, kl, width), F32),
            pltpu.VMEM((CHUNKS, 2, piece, width), BF16),
            pltpu.VMEM((CHUNKS, 2, piece, width), BF16),
            pltpu.VMEM((CHUNKS, 2, 2, piece, width), BF16),
            pltpu.VMEM((CHUNKS, 2, 2, piece, width), BF16),
            pltpu.VMEM((CHUNKS, 2, piece, width), BF16),
            pltpu.VMEM((PARTS, NZ - 1, piece, width), BF16),
            pltpu.VMEM((PARTS, piece, width), BF16),
            pltpu.SemaphoreType.DMA((1 + PARTS,)),
            pltpu.SemaphoreType.DMA((10,)),
            pltpu.SemaphoreType.DMA((CHUNKS * 14,)),
        ],
        compiler_params=pltpu.CompilerParams(
            collective_id=0, has_side_effects=True, vmem_limit_bytes=60 * 2**20
        ),
    )(t2_amps, l2_amps)


def solution(mesh):
    return jax.shard_map(
        on_device,
        mesh=mesh,
        in_specs=(P("row", "col"), P("row", "col")),
        out_specs=P("row", "col"),
        check_vma=False,
    )
```

time: 297 us -> 79 us (0.27)
  waiting for transfers between devices: 193 us -> 0 us
  Pallas kernels: 0 us -> 77.3 us
  blocking collectives: 73.1 us -> 0 us
  matrix products: 14.7 us -> 0 us
  between operations: 13.2 us -> 0.01 us
    reduce_scatter x2 -> x0, waiting for transfers between devices: 104 us -> none  [own_rows(): subtotal = lax.psum_scatter(subtotal, axis, scatter_dimension=0, tiled=True)]
    all_gather x1 -> x0, waiting for transfers between devices: 87.6 us -> none  [on_device(): lax.all_gather(l2_amps, ROW, axis=0, tiled=True)]
    pallas_call x0 -> x1, Pallas kernels: none -> 77.3 us  [on_device(): pl.pallas_call(kernel, out_shape=jax.ShapeDtypeStruct(l2_amps.shape, BF16...]
    all_to_all x4 -> x0, blocking collectives: 73.1 us -> none  [the longest x1 33.2 us: sum_by_axis(): return jnp.sum(lax.all_to_all(own, far, 0, 0, tiled=True), axis=0)]
    dot_general x2 -> x0, matrix products: 14.7 us -> none  [the longest x1 8.19 us: on_device(): lax.dot_general(oooo_half, t2_amps, (((0,), (0,)), ((), ())), preferred_e...]
  transfers between devices with their start and end apart: 3 -> 0, of which waited for: 3 -> 0; matrix products, arithmetic and copies ran while one was open for 0% -> 0% of each run, Pallas kernels for 0% -> 0%
where the time goes in v2:
time: 79 us; the launch traced here: 78.9 us
  Pallas kernels  77.3 us (98%)
  local copies, waits for them, and re-layouts  1.62 us (2%)
    pallas_call x1, Pallas kernels, on_device(): pl.pallas_call(kernel, out_shape=jax.ShapeDtypeStruct(l2_amps.shape, BF16...  77.3 us
    unnamed x1, local copies, waits for them, and re-layouts  1.62 us

profile of v2, /device:TPU:1, one launch (start us, length us, event | category | flops | bytes accessed | tf_op | source)
XLA Modules:
  0.0 78.9 jit_solution(16050714271622653270)
XLA Ops:
  0.0 77.3 %shard_map.28 = bf16[32,3072]{1,0:T(8,128)(2,1)} custom-call(bf16[1024,3072]{1,0:T(8,128)(2,1)} %t2_hbm.1, bf16[32,3072]{1,0:T(8,128)(2,1)} %l2_hbm.1), custom_call_target="tpu_custom_call" | custom-call | tf_op jit(solution)/shard_map/pallas_call | solution.py:263
  77.3 1.6 %copy.4 = bf16[32,3072]{1,0:T(8,128)(2,1)} copy(bf16[32,3072]{1,0:T(8,128)(2,1)} %shard_map.28) | data formatting | bytes 393216

commit v3 on v2

--- a/solution.py
+++ b/solution.py
@@ -14,34 +14,34 @@
 FAR_TYPE = BF16
 
 ORDER = (
-    "ob0 ox1 ox0 ox3",
-    "oa0 f10 oa1 f30",
-    "tt1 tt3 ox2 ob1",
+    "ob0 ox0 ox1 ox3",
+    "oa0 tt1 f10 ob1",
+    "f30 ox2 tt3 oa1",
     "tt0 f20 rl1 oa2",
-    "tt2 f21 rl0 f31",
-    "f11 ob2 ma1 rl2",
-    "ys1 oa3 f22 ma0",
-    "rl3 f32 ys0 ob3",
-    "f12 ma2 rl4 yq1",
-    "ys2 f23 ma3 yq0",
-    "rl5 f13 f33 ys3",
-    "ma4 rl6 yq2 zq1",
-    "ys4 ma5 zq0 yq3",
-    "rl7 ys5 ma6 zq2",
-    "ca1 yq4 ys6 ca0",
-    "ma7 mm0 ys7 yq5",
-    "ca2 zq3 bf0 mm1",
-    "mm2 yq6 zq4 bf2",
-    "bd0 yq7 bf1 ca3",
-    "zq5 bd1 ca4 bd2",
-    "mm3 mm4 bs0 bf4",
-    "zq6 ca5 zq7 bf3",
-    "bs1 bd3 mm5 bd4",
-    "bf5 ca6 ca7 bs2",
-    "mm6 mm7 bs4 bd5",
-    "ou0 bs3 bf6 bd6",
-    "bf7 bs5 bd7 bs6",
-    "bs7 ou2 ou1 ou3",
+    "f11 tt2 f31 rl0",
+    "f21 ob2 ma1 rl3",
+    "f22 oa3 ys1 ma0",
+    "rl2 f12 ob3 f32",
+    "ys0 ma3 yq1 rl4",
+    "ys3 f23 ma2 yq0",
+    "rl5 f33 ys2 ma4",
+    "zq1 yq3 rl6 f13",
+    "ys4 ma5 yq2 zq0",
+    "ca1 ys5 ma6 rl7",
+    "yq4 mm1 ca0 zq3",
+    "ys6 bf1 mm0 yq5",
+    "zq2 bf0 ma7 bd1",
+    "ca3 zq4 ys7 yq6",
+    "bd0 mm3 ca2 bf3",
+    "zq5 ca4 mm2 yq7",
+    "bf2 mm4 zq6 ca5",
+    "bs1 bd3 bd2 mm5",
+    "ca6 bf4 zq7 bs3",
+    "bd4 mm6 bs2 bf5",
+    "bf6 bd5 ca7 bs4",
+    "bs0 mm7 bd6 bf7",
+    "bs5 bd7 ou1 bs6",
+    "bs7 ou0 ou2 ou3",
 )
 
 

time: 79 us -> 77.9 us (0.986)
  Pallas kernels: 77.3 us -> 76 us
    pallas_call x1, Pallas kernels: 77.3 us -> 76 us  [on_device(): pl.pallas_call(kernel, out_shape=jax.ShapeDtypeStruct(l2_amps.shape, BF16...]
where the time goes in v3:
time: 77.9 us; the launch traced here: 77.6 us
  Pallas kernels  76 us (98%)
  local copies, waits for them, and re-layouts  1.62 us (2%)
    pallas_call x1, Pallas kernels, on_device(): pl.pallas_call(kernel, out_shape=jax.ShapeDtypeStruct(l2_amps.shape, BF16...  76 us
    unnamed x1, local copies, waits for them, and re-layouts  1.62 us

profile of v3, /device:TPU:1, one launch (start us, length us, event | category | flops | bytes accessed | tf_op | source)
XLA Modules:
  0.0 77.6 jit_solution(17468268798474812934)
XLA Ops:
  0.0 76.0 %shard_map.28 = bf16[32,3072]{1,0:T(8,128)(2,1)} custom-call(bf16[1024,3072]{1,0:T(8,128)(2,1)} %t2_hbm.1, bf16[32,3072]{1,0:T(8,128)(2,1)} %l2_hbm.1), custom_call_target="tpu_custom_call" | custom-call | tf_op jit(solution)/shard_map/pallas_call | solution.py:263
  76.0 1.6 %copy.4 = bf16[32,3072]{1,0:T(8,128)(2,1)} copy(bf16[32,3072]{1,0:T(8,128)(2,1)} %shard_map.28) | data formatting | bytes 393216

commit v4 on v3

--- a/solution.py
+++ b/solution.py
@@ -14,40 +14,40 @@
 FAR_TYPE = BF16
 
 ORDER = (
-    "ob0 ox0 ox1 ox3",
-    "oa0 tt1 f10 ob1",
-    "f30 ox2 tt3 oa1",
-    "tt0 f20 rl1 oa2",
-    "f11 tt2 f31 rl0",
-    "f21 ob2 ma1 rl3",
-    "f22 oa3 ys1 ma0",
-    "rl2 f12 ob3 f32",
-    "ys0 ma3 yq1 rl4",
-    "ys3 f23 ma2 yq0",
-    "rl5 f33 ys2 ma4",
-    "zq1 yq3 rl6 f13",
-    "ys4 ma5 yq2 zq0",
-    "ca1 ys5 ma6 rl7",
-    "yq4 mm1 ca0 zq3",
-    "ys6 bf1 mm0 yq5",
-    "zq2 bf0 ma7 bd1",
-    "ca3 zq4 ys7 yq6",
-    "bd0 mm3 ca2 bf3",
-    "zq5 ca4 mm2 yq7",
-    "bf2 mm4 zq6 ca5",
-    "bs1 bd3 bd2 mm5",
-    "ca6 bf4 zq7 bs3",
-    "bd4 mm6 bs2 bf5",
-    "bf6 bd5 ca7 bs4",
-    "bs0 mm7 bd6 bf7",
-    "bs5 bd7 ou1 bs6",
-    "bs7 ou0 ou2 ou3",
+    "ob1 ox2 ox0 ox1",
+    "ob0 tt1 tt0 f11",
+    "oa3 f31 f10 f30",
+    "oa0 rl3 ox3 tt3",
+    "oa1 f23 oa2 rl1",
+    "tt2 f20 ma3 ob3",
+    "rl6 f21 ys3 ma1",
+    "rl0 ob2 f13 f22",
+    "ys1 ma6 rl2 yq3",
+    "ys6 f12 ma0 f32",
+    "yq1 ys0 rl4 f33",
+    "ma2 yq6 zq3 rl5",
+    "ys2 ma4 yq0 zq1",
+    "rl7 ca3 ys4 ma5",
+    "yq2 zq6 mm3 ys5",
+    "ca1 bf3 ma7 zq0",
+    "mm1 yq4 ys7 bd3",
+    "ca6 bf1 yq5 zq2",
+    "mm6 bf6 bd1 ca0",
+    "yq7 mm0 ca2 zq4",
+    "bf0 mm2 bd6 zq5",
+    "bf2 bd0 bs3 ca4",
+    "zq7 mm4 bd2 bf4",
+    "bs1 ca5 bs6 mm5",
+    "ca7 bs0 bd4 mm7",
+    "bs2 bf5 bd5 bs4",
+    "bf7 bd7 bs5 ou1",
+    "bs7 ou2 ou0 ou3",
 )
 
 
 def kernel(
-    t2_hbm, l2_hbm, out_hbm,
-    t2, t2t, g, p, rc, sy, ry, q, sz, rz, h, lad, xas, xa, xbs, xb, zs, zb, out,
+    t2_hbm, l2_hbm, out_ref,
+    t2, t2t, g, p, rc, sy, ry, q, sz, rz, h, lad, xas, xa, xbs, xb, zs, zb,
     local, send_sems, sems,
 ):
     rows, width = t2.shape
@@ -86,7 +86,13 @@
 
     names = {}
 
+    words = " ".join(ORDER).split()
+    last = max(range(CHUNKS), key=lambda k: words.index(f"bs{k}"))
     count = [0]
+
+    def cuts(k):
+        n = 2 if k == last else 1
+        return [pl.ds(s * (width // n), width // n) for s in range(n)]
 
     def index(name, size=1):
         if name not in names:
@@ -198,8 +204,11 @@
         own = h.at[k, c]
         send("ca", index(("ca", k)), own, own, partner)
 
+    def ladder_at(group, slot_z):
+        return pl.ds((group % NX) * (2 * piece) + slot_z * piece, piece)
+
     def ladder_rows(k, group, slot_z):
-        return lad[k, pl.ds((group % NX) * (2 * piece) + slot_z * piece, piece), :]
+        return lad[k, ladder_at(group, slot_z), :]
 
     def mm(k):
         arrived(index(("ca", k)), h.at[k, 1 - c])
@@ -211,39 +220,45 @@
     def bf(k):
         for way in range(2):
             xbs[k, 1 - way, way] = ladder_rows(k, x + (1 if way == 0 else 3), 1 - way).astype(BF16)
-            send("b", index(("b", k, 1 - way)), xbs.at[k, 1 - way, way], xb.at[k, 1 - way, way], x_peer(way))
+            for s, at_s in enumerate(cuts(k)):
+                send_b(k, 1 - way, way, s, at_s)
+
+    def send_b(k, slot_z, way, s, at_s):
+        send("b", index(("b", k, slot_z, s)), xbs.at[k, slot_z, way, :, at_s], xb.at[k, slot_z, way, :, at_s], x_peer(way))
 
     def bd(k):
         for way in range(2):
             arrived(index(("a", k, way)), xa.at[k, way])
-            total = ladder_rows(k, x + (1 if way == 0 else 3), way) + xa[k, way].astype(F32)
-            xbs[k, way, way] = total.astype(BF16)
-            send("b", index(("b", k, way)), xbs.at[k, way, way], xb.at[k, way, way], x_peer(way))
+        for s, at_s in enumerate(cuts(k)):
+            for way in range(2):
+                mine = lad[k, ladder_at(x + (1 if way == 0 else 3), way), at_s]
+                xbs[k, way, way, :, at_s] = (mine + xa[k, way, :, at_s].astype(F32)).astype(BF16)
+                send_b(k, way, way, s, at_s)
 
     def bs(k):
-        for slot_z in range(2):
-            arrived(index(("b", k, slot_z)), xb.at[k, slot_z])
-            total = ladder_rows(k, x, slot_z) + xb[k, slot_z, 0].astype(F32) + xb[k, slot_z, 1].astype(F32)
-            if k % 2 == 0:
-                lad[k, pl.ds(x * (2 * piece) + slot_z * piece, piece), :] = total
-            zs[k, slot_z] = total.astype(BF16)
-        for d in (2,) if k % 2 == 0 else (1, 3):
-            send("zr", index(("zr", k // 2)), zs.at[k, ((z + d) % NZ) // 2], zb.at[k // 2, d - 1], z_peer(d))
-
-    stores = []
+        for s, at_s in enumerate(cuts(k)):
+            for slot_z in range(2):
+                arrived(index(("b", k, slot_z, s)), xb.at[k, slot_z, :, :, at_s])
+                at_x = ladder_at(x, slot_z)
+                total = lad[k, at_x, at_s] + xb[k, slot_z, 0, :, at_s].astype(F32) + xb[k, slot_z, 1, :, at_s].astype(F32)
+                if k % 2 == 0:
+                    lad[k, at_x, at_s] = total
+                zs[k, slot_z, :, at_s] = total.astype(BF16)
+            for d in (2,) if k % 2 == 0 else (1, 3):
+                send(
+                    "zr", index(("zr", k // 2)), zs.at[k, ((z + d) % NZ) // 2, :, at_s],
+                    zb.at[k // 2, d - 1, :, at_s], z_peer(d),
+                )
 
     def ou(j):
         arrived(index(("zr", j)), zb.at[j])
         total = ladder_rows(2 * j, x, zz)
         for d in range(3):
             total += zb[j, d].astype(F32)
-        out[j] = total.astype(BF16)
-        store = pltpu.make_async_copy(out.at[j], out_hbm.at[pl.ds(j * piece, piece)], local.at[j])
-        store.start()
-        stores.append(store)
+        out_ref[pl.ds(j * piece, piece), :] = total.astype(BF16)
 
     events = dict(oa=oa, ob=ob, tt=tt, ox=ox, f1=f1, f2=f2, f3=f3, rl=rl, ma=ma, ys=ys, yq=yq, zq=zq, ca=ca, mm=mm, bf=bf, bd=bd, bs=bs, ou=ou)
-    for name in " ".join(ORDER).split():
+    for name in words:
         with jax.named_scope(name):
             events[name[:2]](int(name[2:]))
     with jax.named_scope("drain"):
@@ -252,8 +267,6 @@
         )
         for kind in kinds:
             waiting(kind, 0, sent[kind]).wait_send()
-        for store in stores:
-            store.wait()
 
 
 def on_device(t2_amps, l2_amps):
@@ -262,9 +275,9 @@
     kl = NX * 2 * piece
     return pl.pallas_call(
         kernel,
-        out_shape=jax.ShapeDtypeStruct(l2_amps.shape, BF16),
+        out_shape=pltpu.VMEM(l2_amps.shape, BF16),
         in_specs=[pl.BlockSpec(memory_space=pl.ANY)] * 2,
-        out_specs=pl.BlockSpec(memory_space=pl.ANY),
+        out_specs=pl.BlockSpec(memory_space=pltpu.VMEM),
         scratch_shapes=[
             pltpu.VMEM((rows, width), BF16),
             pltpu.VMEM((width, rows), BF16),
@@ -284,15 +297,14 @@
             pltpu.VMEM((CHUNKS, 2, 2, piece, width), BF16),
             pltpu.VMEM((CHUNKS, 2, piece, width), BF16),
             pltpu.VMEM((PARTS, NZ - 1, piece, width), BF16),
-            pltpu.VMEM((PARTS, piece, width), BF16),
             pltpu.SemaphoreType.DMA((1 + PARTS,)),
             pltpu.SemaphoreType.DMA((10,)),
-            pltpu.SemaphoreType.DMA((CHUNKS * 14,)),
+            pltpu.SemaphoreType.DMA((CHUNKS * 14 + 2,)),
         ],
         compiler_params=pltpu.CompilerParams(
-            collective_id=0, has_side_effects=True, vmem_limit_bytes=60 * 2**20
+            collective_id=0, has_side_effects=True, vmem_limit_bytes=52 * 2**20
         ),
-    )(t2_amps, l2_amps)
+    )(*(pltpu.with_memory_space_constraint(v, pltpu.HBM) for v in (t2_amps, l2_amps)))
 
 
 def solution(mesh):

time: 77.9 us -> 76.8 us (0.986)
  local copies, waits for them, and re-layouts: 1.62 us -> 0.68 us
    unnamed x1, local copies, waits for them, and re-layouts: 1.62 us -> 0.68 us
where the time goes in v4:
time: 76.8 us; the launch traced here: 76.7 us
  Pallas kernels  76 us (99%)
    pallas_call x1, Pallas kernels, on_device(): pl.pallas_call(kernel, out_shape=pltpu.VMEM(l2_amps.shape, BF16), in_spec...  76 us

profile of v4, /device:TPU:1, one launch (start us, length us, event | category | flops | bytes accessed | tf_op | source)
XLA Modules:
  0.0 76.7 jit_solution(13152445606379017058)
XLA Ops:
  0.0 76.0 %shard_map.28 = bf16[32,3072]{1,0:T(8,128)(2,1)S(1)} custom-call(bf16[1024,3072]{1,0:T(8,128)(2,1)} %t2_hbm.1, bf16[32,3072]{1,0:T(8,128)(2,1)} %l2_hbm.1), custom_call_target="tpu_custom_call" | custom-call | tf_op jit(solution)/shard_map/pallas_call | solution.py:276
  76.0 0.7 copy.4

commit v5 on v4

--- a/solution.py
+++ b/solution.py
@@ -14,34 +14,34 @@
 FAR_TYPE = BF16
 
 ORDER = (
-    "ob1 ox2 ox0 ox1",
-    "ob0 tt1 tt0 f11",
-    "oa3 f31 f10 f30",
-    "oa0 rl3 ox3 tt3",
-    "oa1 f23 oa2 rl1",
-    "tt2 f20 ma3 ob3",
-    "rl6 f21 ys3 ma1",
-    "rl0 ob2 f13 f22",
-    "ys1 ma6 rl2 yq3",
-    "ys6 f12 ma0 f32",
-    "yq1 ys0 rl4 f33",
-    "ma2 yq6 zq3 rl5",
-    "ys2 ma4 yq0 zq1",
-    "rl7 ca3 ys4 ma5",
-    "yq2 zq6 mm3 ys5",
-    "ca1 bf3 ma7 zq0",
-    "mm1 yq4 ys7 bd3",
-    "ca6 bf1 yq5 zq2",
-    "mm6 bf6 bd1 ca0",
-    "yq7 mm0 ca2 zq4",
-    "bf0 mm2 bd6 zq5",
-    "bf2 bd0 bs3 ca4",
-    "zq7 mm4 bd2 bf4",
-    "bs1 ca5 bs6 mm5",
-    "ca7 bs0 bd4 mm7",
-    "bs2 bf5 bd5 bs4",
-    "bf7 bd7 bs5 ou1",
-    "bs7 ou2 ou0 ou3",
+    "ob1 ox1 ox2 ox0",
+    "ox3 tt1 ob0 tt0",
+    "f11 oa3 f31 oa0",
+    "f10 f30 oa1 rl3",
+    "tt3 tt2 f23 oa2",
+    "rl1 f20 ma3 rl6",
+    "ob2 f21 ys3 ma1",
+    "ob3 rl0 f22 ys1",
+    "ma6 rl2 f12 yq3",
+    "ys6 f32 ma0 rl4",
+    "f33 f13 yq1 ys0",
+    "ma2 yq6 zq3 ys2",
+    "rl5 ma4 zq1 yq0",
+    "rl7 ys4 ca3 ma5",
+    "zq6 mm3 bf3 ca1",
+    "yq2 ys5 ma7 yq4",
+    "mm1 zq0 ca6 ys7",
+    "bf1 bd3 mm6 yq5",
+    "zq2 bd1 ca0 bf6",
+    "zq4 mm0 yq7 bs3",
+    "ca2 bf0 bd6 ca4",
+    "bs1 zq5 mm2 bd0",
+    "mm4 bf4 zq7 bs6",
+    "ca5 bd2 mm5 bs0",
+    "bf2 bd4 ca7 mm7",
+    "bd5 bs2 bf5 bf7",
+    "bs4 bd7 bs5 ou0",
+    "ou1 bs7 ou2 ou3",
 )
 
 
@@ -91,7 +91,7 @@
     count = [0]
 
     def cuts(k):
-        n = 2 if k == last else 1
+        n = 3 if k == last else 1
         return [pl.ds(s * (width // n), width // n) for s in range(n)]
 
     def index(name, size=1):
@@ -299,7 +299,7 @@
             pltpu.VMEM((PARTS, NZ - 1, piece, width), BF16),
             pltpu.SemaphoreType.DMA((1 + PARTS,)),
             pltpu.SemaphoreType.DMA((10,)),
-            pltpu.SemaphoreType.DMA((CHUNKS * 14 + 2,)),
+            pltpu.SemaphoreType.DMA((CHUNKS * 14 + 4,)),
         ],
         compiler_params=pltpu.CompilerParams(
             collective_id=0, has_side_effects=True, vmem_limit_bytes=52 * 2**20

time: 76.8 us -> 76 us (0.990)
  Pallas kernels: 76 us -> 75.2 us
    pallas_call x1, Pallas kernels: 76 us -> 75.2 us  [on_device(): pl.pallas_call(kernel, out_shape=pltpu.VMEM(l2_amps.shape, BF16), in_spec...]
where the time goes in v5:
time: 76 us; the launch traced here: 75.9 us
  Pallas kernels  75.2 us (99%)
    pallas_call x1, Pallas kernels, on_device(): pl.pallas_call(kernel, out_shape=pltpu.VMEM(l2_amps.shape, BF16), in_spec...  75.2 us

profile of v5, /device:TPU:1, one launch (start us, length us, event | category | flops | bytes accessed | tf_op | source)
XLA Modules:
  0.0 75.9 jit_solution(7562985059446022054)
XLA Ops:
  0.0 75.2 %shard_map.28 = bf16[32,3072]{1,0:T(8,128)(2,1)S(1)} custom-call(bf16[1024,3072]{1,0:T(8,128)(2,1)} %t2_hbm.1, bf16[32,3072]{1,0:T(8,128)(2,1)} %l2_hbm.1), custom_call_target="tpu_custom_call" | custom-call | tf_op jit(solution)/shard_map/pallas_call | solution.py:276
  75.2 0.7 copy.4
